TPU v7x, 256 devices: a whole 4x4x8 slice. The times are simulated.
256 devices in a mesh: gx: 8 (over x, z_hi), gy: 8 (over z_lo, core), gz: 4 (over y).
Axes of the slice: x: 4, y: 4, z: 8 (z_hi: 2, z_lo: 4; z = z_hi * 4 + z_lo), core: 2. Of those that a mesh axis runs over, the one named last changes fastest.
Arguments:
- section_state: float32 [25, 64, 128, 512], P(None, 'gx', 'gy', 'gz'), may hold values from -6 to 6
- step_start: float32 [25, 64, 128, 512], P(None, 'gx', 'gy', 'gz'), may hold values from -6 to 6
- weighted_sum: float32 [25, 64, 128, 512], P(None, 'gx', 'gy', 'gz'), may hold values from -6 to 6
- upwind_sign: int32 [3, 64, 128, 512], P(None, 'gx', 'gy', 'gz'), may hold values 0 or 1
Outputs:
- next_section: float32 [25, 64, 128, 512], P(None, 'gx', 'gy', 'gz')
- new_weighted: float32 [25, 64, 128, 512], P(None, 'gx', 'gy', 'gz')
Inputs may be any that keep to these rules, and one draw needn't show every extreme that they name: upwind_sign[k] is 1 where the advection stencil along dimension k leans toward higher indices and 0 where it leans toward lower ones.
All inputs are finite; a program needn't handle non-finite values. No bound on the sum of `upwind_sign` on one device may be relied on, other than what follows from the above.
Results may differ from a plain program's by a relative error of at most 0.00002.
Values sent between devices are 32-bit elements; how exact they have to be, the bound alone decides.
A program may use at most 64 MiB of HBM per device.

v0:
```python
import functools

import jax
import jax.numpy as jnp
from jax import lax
from jax.experimental import pallas as pl
from jax.experimental.pallas import tpu as pltpu
from jax.sharding import PartitionSpec as P

MESH = pl.DeviceIdType.MESH

special = (0, 18, 19, 20, 21)
early_runs = ((18, 4), (0, 1))
middle_runs = ((14, 4), (7, 1), (1, 6))
late_runs = ((8, 6), (22, 3))
runs = early_runs + middle_runs + late_runs
sym_pairs = ((0, 0), (0, 1), (0, 2), (1, 1), (1, 2), (2, 2))
kappa_one = 0.5
damping = 2.0
dissipation = 0.3
time_step = 0.25

LAYERS = 14
ROWS = 32


def first_diff(at):
    return ((at(-2) - at(2)) + 8.0 * (at(1) - at(-1))) * (1.0 / 12.0)


def second_diff(at):
    return (16.0 * (at(-1) + at(1)) - (at(-2) + at(2)) - 30.0 * at(0)) * (1.0 / 12.0)


def drift(at, odd_weight, even_weight):
    sums = [at(m) + at(-m) for m in (1, 2, 3)]
    gaps = [at(m) - at(-m) for m in (1, 2, 3)]
    odd = gaps[2] - 6.0 * gaps[1] + 21.0 * gaps[0]
    even = sums[2] - 6.0 * sums[1] + 15.0 * sums[0] - 20.0 * at(0)
    return odd_weight * odd + even_weight * even


def kernel(
    sizes,
    state,
    sign,
    rates,
    cells,
    wrap,
    lean,
    weights,
    diff_y,
    diff_z,
    y_out,
    y_in,
    z_out,
    z_in,
    y_out2,
    y_in2,
    z_out2,
    z_in2,
    x_sent,
    x_got,
    n_sent,
    n_got,
    local,
):
    here = {axis: lax.axis_index(axis) for axis in sizes}

    def beside(axis, step):
        return {axis: lax.rem(here[axis] + step + sizes[axis], sizes[axis])}

    barrier = pltpu.get_barrier_semaphore()
    for axis in sizes:
        for step in (1, -1):
            pl.semaphore_signal(barrier, inc=1, device_id=beside(axis, step), device_id_type=MESH)
    own = pltpu.make_async_copy(state, cells.at[:, pl.ds(3, 8), pl.ds(8, 16)], local.at[0])
    own.start()
    leaning = pltpu.make_async_copy(sign, lean, local.at[1])
    leaning.start()

    def x_copy(side, run):
        first, count = runs[run]
        return pltpu.make_async_remote_copy(
            src_ref=state.at[pl.ds(first, count), pl.ds(0 if side else 5, 3)],
            dst_ref=cells.at[pl.ds(first, count), pl.ds(11 if side else 0, 3), pl.ds(8, 16)],
            send_sem=x_sent.at[side, run],
            recv_sem=x_got.at[side, run],
            device_id=beside("gx", -1 if side else 1),
            device_id_type=MESH,
        )

    def n_copy(which, side):
        axis, out, got = (
            ("gy", y_out, y_in),
            ("gz", z_out, z_in),
            ("gy", y_out2, y_in2),
            ("gz", z_out2, z_in2),
        )[which]
        return pltpu.make_async_remote_copy(
            src_ref=out.at[side],
            dst_ref=got.at[side],
            send_sem=n_sent.at[which, side],
            recv_sem=n_got.at[which, side],
            device_id=beside(axis, -1 if side else 1),
            device_id_type=MESH,
        )

    def x_start(chosen):
        for run in chosen:
            for side in (0, 1):
                x_copy(side, run).start()

    def x_wait(chosen):
        for run in chosen:
            for side in (0, 1):
                x_copy(side, run).wait_recv()

    def n_start(which):
        for side in (0, 1):
            n_copy(which, side).start()

    def n_wait(which):
        for side in (0, 1):
            n_copy(which, side).wait_recv()

    at_early = range(len(early_runs))
    at_middle = range(len(early_runs), len(early_runs) + len(middle_runs))
    at_late = range(len(early_runs) + len(middle_runs), len(runs))

    pl.semaphore_wait(barrier, 2 * len(sizes))
    x_start(at_early)

    own.wait()
    leaning.wait()

    @pl.loop(0, 25)
    def _(f):
        for r in range(3):
            y_out[0, f, r] = cells[f, pl.ds(3, 8), 21 + r]
            y_out[1, f, r] = cells[f, pl.ds(3, 8), 8 + r]

    @pl.loop(0, 25)
    def _(f):
        turned = cells[f, pl.ds(3, 8), pl.ds(8, 16)].reshape(128, 128).T
        z_out[0, f] = turned[120:128]
        z_out[1, f] = turned[0:8]

    n_start(0)

    @pl.loop(0, 8)
    def _(i):
        for k in range(3):
            scaled = cells[19 + k, 3 + i, pl.ds(8, 16)] * (1.0 / 24.0)
            weights[k, i] = scaled
            weights[3 + k, i] = dissipation / 64.0 + jnp.where(lean[k, i] == 1, scaled, -scaled)

    n_start(1)
    x_start(at_middle)

    lane = lax.broadcasted_iota(jnp.int32, (16, 128), 1)
    lane8 = lax.broadcasted_iota(jnp.int32, (8, 128), 1)

    def along_z(field, layer, start, count):
        inside = cells[field, layer, pl.ds(start, count)]
        outside = wrap[field, layer, pl.ds(start, count)]
        lanes = lane if count == 16 else lane8

        def at(m):
            if m == 0:
                return inside
            if m > 0:
                return pltpu.roll(jnp.where(lanes < m, outside, inside), 128 - m, 1)
            return pltpu.roll(jnp.where(lanes >= 128 + m, outside, inside), -m, 1)

        return at

    def along_y(field, i):
        return lambda m: cells[field, 3 + i, pl.ds(8 + m, 16)]

    def along_x(field, i):
        return lambda m: cells[field, 3 + i + m, pl.ds(8, 16)]

    def turned_back(low, high):
        return jnp.concatenate([high, jnp.zeros((112, 128), jnp.float32), low], axis=0).T

    n_wait(0)

    @pl.loop(0, 25)
    def _(f):
        for r in range(3):
            cells[f, pl.ds(3, 8), 5 + r] = y_in[0, f, r]
            cells[f, pl.ds(3, 8), 24 + r] = y_in[1, f, r]

    n_wait(1)

    @pl.loop(0, 25)
    def _(f):
        wrap[f, pl.ds(3, 8), pl.ds(8, 16)] = turned_back(z_in[0, f], z_in[1, f]).reshape(8, 16, 128)

    x_wait(at_early)
    for n, f in enumerate(special):
        for q, layer in enumerate((1, 2, 11, 12)):
            y_out2[0, n, pl.ds(2 * q, 2)] = cells[f, layer, pl.ds(22, 2)]
            y_out2[1, n, pl.ds(2 * q, 2)] = cells[f, layer, pl.ds(8, 2)]
        turned = jnp.concatenate(
            [
                cells[f, pl.ds(1, 2), pl.ds(8, 16)].reshape(32, 128),
                cells[f, pl.ds(11, 2), pl.ds(8, 16)].reshape(32, 128),
                y_in[0, f, 1],
                y_in[0, f, 2],
                y_in[1, f, 0],
                y_in[1, f, 1],
                jnp.zeros((32, 128), jnp.float32),
            ],
            axis=0,
        ).T
        z_out2[0, n] = turned[120:128]
        z_out2[1, n] = turned[0:8]

    @pl.loop(0, 25)
    def _(f):
        @pl.loop(0, 8)
        def _(i):
            rates[f, i] = drift(along_y(f, i), weights[1, i], weights[4, i]) + drift(
                along_z(f, 3 + i, 8, 16), weights[2, i], weights[5, i]
            )

    n_start(2)
    n_start(3)
    x_start(at_late)

    def drift_x(first, count):
        @pl.loop(first, first + count)
        def _(f):
            @pl.loop(0, 8)
            def _(i):
                rates[f, i] += drift(along_x(f, i), weights[0, i], weights[3, i])

    for run in at_early:
        drift_x(*runs[run])

    n_wait(2)
    n_wait(3)
    for n, f in enumerate(special):
        for q, layer in enumerate((1, 2, 11, 12)):
            cells[f, layer, pl.ds(6, 2)] = y_in2[0, n, pl.ds(2 * q, 2)]
            cells[f, layer, pl.ds(24, 2)] = y_in2[1, n, pl.ds(2 * q, 2)]
        back = turned_back(z_in2[0, n], z_in2[1, n])
        wrap[f, pl.ds(1, 2), pl.ds(8, 16)] = back[0:32].reshape(2, 16, 128)
        wrap[f, pl.ds(11, 2), pl.ds(8, 16)] = back[32:64].reshape(2, 16, 128)
        for q, row in enumerate((6, 7, 24, 25)):
            wrap[f, pl.ds(3, 8), row] = back[64 + 8 * q : 72 + 8 * q]
        for layer in range(1, 13):
            diff_y[n, layer] = first_diff(lambda m: cells[f, layer, pl.ds(8 + m, 16)])
            diff_z[n, layer, pl.ds(8, 16)] = first_diff(along_z(f, layer, 8, 16))
        for layer in range(3, 11):
            diff_z[n, layer, pl.ds(0, 8)] = first_diff(along_z(f, layer, 0, 8))
            diff_z[n, layer, pl.ds(24, 8)] = first_diff(along_z(f, layer, 24, 8))

    for run in at_middle:
        x_wait([run])
        drift_x(*runs[run])

    @pl.loop(0, 8)
    def _(i):
        layer = 3 + i

        def centre(field):
            return cells[field, layer, pl.ds(8, 16)]

        def along(field, k):
            return (along_x(field, i), along_y(field, i), along_z(field, layer, 8, 16))[k]

        def grad(field, k):
            if field in special and k > 0:
                n = special.index(field)
                return diff_y[n, layer] if k == 1 else diff_z[n, layer, pl.ds(8, 16)]
            return first_diff(along(field, k))

        def hess(field, k, l):
            n = special.index(field)
            if k == l:
                return second_diff(along(field, k))
            if (k, l) == (0, 1):
                return first_diff(lambda m: diff_y[n, layer + m])
            if (k, l) == (0, 2):
                return first_diff(lambda m: diff_z[n, layer + m, pl.ds(8, 16)])
            return first_diff(lambda m: diff_z[n, layer, pl.ds(8 + m, 16)])

        def add(field, value):
            rates[field, i] += value

        grad_shift = [[grad(19 + m, k) for k in range(3)] for m in range(3)]
        diverge = grad_shift[0][0] + grad_shift[1][1] + grad_shift[2][2]
        add(0, 2.0 / 3.0 * (centre(7) - diverge))
        for s, (p, q) in enumerate(sym_pairs):
            value = -2.0 * centre(8 + s) + grad_shift[q][p] + grad_shift[p][q]
            if p == q:
                value = value - 2.0 / 3.0 * diverge
            add(1 + s, value)
        add(18, -2.0 * centre(7))
        for p in range(3):
            add(19 + p, 0.75 * centre(22 + p))
        hess_shift = [{pair: hess(19 + m, *pair) for pair in sym_pairs} for m in range(3)]
        for p in range(3):
            lap_shift = hess_shift[p][0, 0] + hess_shift[p][1, 1] + hess_shift[p][2, 2]
            grad_div = hess_shift[0][0, p] + hess_shift[1][min(1, p), max(1, p)] + hess_shift[2][p, 2]
            drive = -(4.0 / 3.0) * grad(7, p) + lap_shift + 1.0 / 3.0 * grad_div
            add(14 + p, drive)
            add(22 + p, drive - damping * centre(22 + p))
        hess_chi = {pair: hess(0, *pair) for pair in sym_pairs}
        hess_lapse = {pair: hess(18, *pair) for pair in sym_pairs}
        lap_chi = hess_chi[0, 0] + hess_chi[1, 1] + hess_chi[2, 2]
        lap_lapse = hess_lapse[0, 0] + hess_lapse[1, 1] + hess_lapse[2, 2]
        add(7, -lap_lapse + kappa_one * centre(17))
        grad_gamma = [[grad(14 + m, k) for k in range(3)] for m in range(3)]
        ricci = []
        for s, (p, q) in enumerate(sym_pairs):
            lap_metric = second_diff(along(1 + s, 0)) + second_diff(along(1 + s, 1)) + second_diff(along(1 + s, 2))
            value = -0.5 * lap_metric + 0.5 * (grad_gamma[q][p] + grad_gamma[p][q]) + 0.5 * hess_chi[p, q]
            if p == q:
                value = value + 0.5 * lap_chi
            ricci.append(value)
        bare = [ricci[s] - hess_lapse[pair] for s, pair in enumerate(sym_pairs)]
        trace = bare[0] + bare[3] + bare[5]
        for s, (p, q) in enumerate(sym_pairs):
            add(8 + s, bare[s] - 1.0 / 3.0 * trace if p == q else bare[s])
        add(17, 0.5 * (ricci[0] + ricci[3] + ricci[5]) - 2.0 * kappa_one * centre(17))

    for run in at_late:
        x_wait([run])
        drift_x(*runs[run])

    for run in range(len(runs)):
        for side in (0, 1):
            x_copy(side, run).wait_send()
    for which in range(4):
        for side in (0, 1):
            n_copy(which, side).wait_send()


def rates_of(sizes, state, sign):
    block = (8, 16, 128)
    f32 = jnp.float32
    return pl.pallas_call(
        functools.partial(kernel, sizes),
        out_shape=jax.ShapeDtypeStruct((25,) + block, f32),
        in_specs=[pl.BlockSpec(memory_space=pl.ANY)] * 2,
        out_specs=pl.BlockSpec(memory_space=pltpu.VMEM),
        scratch_shapes=[
            pltpu.VMEM((25, LAYERS, ROWS, 128), f32),
            pltpu.VMEM((25, LAYERS, ROWS, 128), f32),
            pltpu.VMEM((3,) + block, jnp.int32),
            pltpu.VMEM((6,) + block, f32),
            pltpu.VMEM((5, LAYERS, 16, 128), f32),
            pltpu.VMEM((5, LAYERS, ROWS, 128), f32),
            pltpu.VMEM((2, 25, 3, 8, 128), f32),
            pltpu.VMEM((2, 25, 3, 8, 128), f32),
            pltpu.VMEM((2, 25, 8, 128), f32),
            pltpu.VMEM((2, 25, 8, 128), f32),
            pltpu.VMEM((2, 5, 8, 128), f32),
            pltpu.VMEM((2, 5, 8, 128), f32),
            pltpu.VMEM((2, 5, 8, 128), f32),
            pltpu.VMEM((2, 5, 8, 128), f32),
            pltpu.SemaphoreType.DMA((2, len(runs))),
            pltpu.SemaphoreType.DMA((2, len(runs))),
            pltpu.SemaphoreType.DMA((4, 2)),
            pltpu.SemaphoreType.DMA((4, 2)),
            pltpu.SemaphoreType.DMA((2,)),
        ],
        compiler_params=pltpu.CompilerParams(
            collective_id=0, has_side_effects=True, vmem_limit_bytes=40 * 2**20
        ),
    )(state, sign)


def solution(mesh):
    placed = P(None, "gx", "gy", "gz")
    sizes = dict(mesh.shape)

    def on_device(section_state, step_start, weighted_sum, upwind_sign):
        rates = rates_of(sizes, section_state, upwind_sign)
        return step_start + time_step / 2.0 * rates, weighted_sum + time_step / 3.0 * rates

    return jax.shard_map(
        on_device, mesh=mesh, in_specs=(placed,) * 4, out_specs=(placed, placed), check_vma=False
    )
```

profile of v0, /device:TPU:1, one launch (start us, length us, event | category | flops | bytes accessed | tf_op | source)
XLA Modules:
  0.0 81.1 jit_solution(12543270521983789751)
XLA Ops:
  0.6 0.0 copy-start
  0.6 1.4 %copy-done = f32[25,8,16,128]{3,2,1,0:T(8,128)S(1)} copy-done((f32[25,8,16,128]{3,2,1,0:T(8,128)S(1)}, f32[25,8,16,128]{3,2,1,0:T(8,128)}, u32[]{:S(2)}) %copy-start) | copy-done | bytes 1638424
  2.1 0.0 copy-start.1
  2.1 0.9 %copy-done.1 = s32[3,8,16,128]{3,2,1,0:T(8,128)S(1)} copy-done((s32[3,8,16,128]{3,2,1,0:T(8,128)S(1)}, s32[3,8,16,128]{3,2,1,0:T(8,128)}, u32[]{:S(2)}) %copy-start.1) | copy-done | bytes 196632
  3.0 0.0 copy-start.2
  3.0 0.0 copy-start.3
  3.0 75.7 %shard_map.59 = f32[25,8,16,128]{3,2,1,0:T(8,128)S(1)} custom-call(f32[25,8,16,128]{3,2,1,0:T(8,128)S(1)} %copy-done, s32[3,8,16,128]{3,2,1,0:T(8,128)S(1)} %copy-done.1), custom_call_target="tpu_custom_call" | custom-call | tf_op jit(solution)/shard_map/pallas_call | solution.py:346
  78.7 0.0 copy-done.2
  78.8 0.0 copy-done.3
  78.8 2.4 %multiply_add_fusion = (f32[25,8,16,128]{3,2,1,0:T(8,128)}, f32[25,8,16,128]{3,2,1,0:T(8,128)}) fusion(f32[25,8,16,128]{3,2,1,0:T(8,128)S(1)} %copy-done.2, f32[25,8,16,128]{3,2,1,0:T(8,128)S(1)} %shard_map.59, f32[25,8,16,128]{3,2,1,0:T(8,128)S(1)} %copy-done.3), kind=kLoop, calls=%fused_computation | loop fusion | flops 1638400 | bytes 8192000 | tf_op jit(solution)/shard_map/add | solution.py:384
Async XLA Ops:
  0.6 1.4 %copy-start = (f32[25,8,16,128]{3,2,1,0:T(8,128)S(1)}, f32[25,8,16,128]{3,2,1,0:T(8,128)}, u32[]{:S(2)}) copy-start(f32[25,8,16,128]{3,2,1,0:T(8,128)} %state.1) | copy-start | bytes 4915204
  2.1 0.9 %copy-start.1 = (s32[3,8,16,128]{3,2,1,0:T(8,128)S(1)}, s32[3,8,16,128]{3,2,1,0:T(8,128)}, u32[]{:S(2)}) copy-start(s32[3,8,16,128]{3,2,1,0:T(8,128)} %sign.1) | copy-start | bytes 589828
  3.0 75.8 %copy-start.2 = (f32[25,8,16,128]{3,2,1,0:T(8,128)S(1)}, f32[25,8,16,128]{3,2,1,0:T(8,128)}, u32[]{:S(2)}) copy-start(f32[25,8,16,128]{3,2,1,0:T(8,128)} %param.6) | copy-start | bytes 4915204
  3.0 75.8 %copy-start.3 = (f32[25,8,16,128]{3,2,1,0:T(8,128)S(1)}, f32[25,8,16,128]{3,2,1,0:T(8,128)}, u32[]{:S(2)}) copy-start(f32[25,8,16,128]{3,2,1,0:T(8,128)} %param.5) | copy-start | bytes 4915204
where the time goes:
time: 82.2 us; the launch traced here: 81.1 us
  Pallas kernels  75.7 us (92%)
  other arithmetic  2.37 us (3%)
  local copies, waits for them, and re-layouts  2.36 us (3%)
    pallas_call x1, Pallas kernels, rates_of(): pl.pallas_call(functools.partial(kernel, sizes), out_shape=jax.ShapeDtype...  75.7 us
    add x1, other arithmetic, on_device(): weighted_sum + time_step / 3.0 * rates  2.37 us
    unnamed x8, local copies, waits for them, and re-layouts  2.36 us

commit v1 on v0

--- a/solution.py
+++ b/solution.py
@@ -43,8 +43,14 @@
 def kernel(
     sizes,
     state,
+    start,
+    before,
     sign,
+    ahead,
+    after,
     rates,
+    first_of,
+    before_of,
     cells,
     wrap,
     lean,
@@ -78,6 +84,10 @@
     own.start()
     leaning = pltpu.make_async_copy(sign, lean, local.at[1])
     leaning.start()
+    bases = [
+        pltpu.make_async_copy(start, first_of, local.at[2]),
+        pltpu.make_async_copy(before, before_of, local.at[3]),
+    ]
 
     def x_copy(side, run):
         first, count = runs[run]
@@ -124,9 +134,9 @@
         for side in (0, 1):
             n_copy(which, side).wait_recv()
 
-    at_early = range(len(early_runs))
-    at_middle = range(len(early_runs), len(early_runs) + len(middle_runs))
-    at_late = range(len(early_runs) + len(middle_runs), len(runs))
+    at_early = list(range(len(early_runs)))
+    at_middle = list(range(len(early_runs), len(early_runs) + len(middle_runs)))
+    at_late = list(range(len(early_runs) + len(middle_runs), len(runs)))
 
     pl.semaphore_wait(barrier, 2 * len(sizes))
     x_start(at_early)
@@ -184,6 +194,8 @@
     def turned_back(low, high):
         return jnp.concatenate([high, jnp.zeros((112, 128), jnp.float32), low], axis=0).T
 
+    for copy in bases:
+        copy.start()
     n_wait(0)
 
     @pl.loop(0, 25)
@@ -197,6 +209,14 @@
     @pl.loop(0, 25)
     def _(f):
         wrap[f, pl.ds(3, 8), pl.ds(8, 16)] = turned_back(z_in[0, f], z_in[1, f]).reshape(8, 16, 128)
+
+    @pl.loop(0, 25)
+    def _(f):
+        @pl.loop(0, 8, unroll=4)
+        def _(i):
+            rates[f, i] = drift(along_y(f, i), weights[1, i], weights[4, i]) + drift(
+                along_z(f, 3 + i, 8, 16), weights[2, i], weights[5, i]
+            )
 
     x_wait(at_early)
     for n, f in enumerate(special):
@@ -218,27 +238,19 @@
         z_out2[0, n] = turned[120:128]
         z_out2[1, n] = turned[0:8]
 
-    @pl.loop(0, 25)
-    def _(f):
-        @pl.loop(0, 8)
-        def _(i):
-            rates[f, i] = drift(along_y(f, i), weights[1, i], weights[4, i]) + drift(
-                along_z(f, 3 + i, 8, 16), weights[2, i], weights[5, i]
-            )
+    def drift_x(first, count):
+        @pl.loop(first, first + count)
+        def _(f):
+            @pl.loop(0, 8, unroll=2)
+            def _(i):
+                rates[f, i] += drift(along_x(f, i), weights[0, i], weights[3, i])
+
+    for run in at_early:
+        drift_x(*runs[run])
 
     n_start(2)
     n_start(3)
     x_start(at_late)
-
-    def drift_x(first, count):
-        @pl.loop(first, first + count)
-        def _(f):
-            @pl.loop(0, 8)
-            def _(i):
-                rates[f, i] += drift(along_x(f, i), weights[0, i], weights[3, i])
-
-    for run in at_early:
-        drift_x(*runs[run])
 
     n_wait(2)
     n_wait(3)
@@ -328,9 +340,31 @@
             add(8 + s, bare[s] - 1.0 / 3.0 * trace if p == q else bare[s])
         add(17, 0.5 * (ricci[0] + ricci[3] + ricci[5]) - 2.0 * kappa_one * centre(17))
 
+    for copy in bases:
+        copy.wait()
+
+    def finish(f, i, value):
+        ahead[f, i] = first_of[f, i] + time_step / 2.0 * value
+        after[f, i] = before_of[f, i] + time_step / 3.0 * value
+
+    for run in at_early + at_middle:
+        first, count = runs[run]
+
+        @pl.loop(first, first + count)
+        def _(f):
+            @pl.loop(0, 8, unroll=4)
+            def _(i):
+                finish(f, i, rates[f, i])
+
     for run in at_late:
         x_wait([run])
-        drift_x(*runs[run])
+        first, count = runs[run]
+
+        @pl.loop(first, first + count)
+        def _(f):
+            @pl.loop(0, 8, unroll=4)
+            def _(i):
+                finish(f, i, rates[f, i] + drift(along_x(f, i), weights[0, i], weights[3, i]))
 
     for run in range(len(runs)):
         for side in (0, 1):
@@ -340,15 +374,19 @@
             n_copy(which, side).wait_send()
 
 
-def rates_of(sizes, state, sign):
+def section_of(sizes, *arrays):
     block = (8, 16, 128)
     f32 = jnp.float32
+    whole = jax.ShapeDtypeStruct((25,) + block, f32)
     return pl.pallas_call(
         functools.partial(kernel, sizes),
-        out_shape=jax.ShapeDtypeStruct((25,) + block, f32),
-        in_specs=[pl.BlockSpec(memory_space=pl.ANY)] * 2,
-        out_specs=pl.BlockSpec(memory_space=pltpu.VMEM),
+        out_shape=(whole, whole),
+        in_specs=[pl.BlockSpec(memory_space=pltpu.HBM)] * 4,
+        out_specs=[pl.BlockSpec(memory_space=pltpu.VMEM)] * 2,
         scratch_shapes=[
+            pltpu.VMEM((25,) + block, f32),
+            pltpu.VMEM((25,) + block, f32),
+            pltpu.VMEM((25,) + block, f32),
             pltpu.VMEM((25, LAYERS, ROWS, 128), f32),
             pltpu.VMEM((25, LAYERS, ROWS, 128), f32),
             pltpu.VMEM((3,) + block, jnp.int32),
@@ -367,12 +405,23 @@
             pltpu.SemaphoreType.DMA((2, len(runs))),
             pltpu.SemaphoreType.DMA((4, 2)),
             pltpu.SemaphoreType.DMA((4, 2)),
-            pltpu.SemaphoreType.DMA((2,)),
+            pltpu.SemaphoreType.DMA((4,)),
         ],
         compiler_params=pltpu.CompilerParams(
             collective_id=0, has_side_effects=True, vmem_limit_bytes=40 * 2**20
         ),
-    )(state, sign)
+    )(*(pltpu.with_memory_space_constraint(x, pltpu.HBM) for x in arrays))
+
+
+def put_out(ahead, after, ahead_out, after_out, sems):
+    copies = [
+        pltpu.make_async_copy(ahead, ahead_out, sems.at[0]),
+        pltpu.make_async_copy(after, after_out, sems.at[1]),
+    ]
+    for copy in copies:
+        copy.start()
+    for copy in copies:
+        copy.wait()
 
 
 def solution(mesh):
@@ -380,8 +429,15 @@
     sizes = dict(mesh.shape)
 
     def on_device(section_state, step_start, weighted_sum, upwind_sign):
-        rates = rates_of(sizes, section_state, upwind_sign)
-        return step_start + time_step / 2.0 * rates, weighted_sum + time_step / 3.0 * rates
+        ahead, after = section_of(sizes, section_state, step_start, weighted_sum, upwind_sign)
+        return pl.pallas_call(
+            put_out,
+            out_shape=(ahead, after),
+            in_specs=[pl.BlockSpec(memory_space=pltpu.VMEM)] * 2,
+            out_specs=[pl.BlockSpec(memory_space=pltpu.HBM)] * 2,
+            scratch_shapes=[pltpu.SemaphoreType.DMA((2,))],
+            compiler_params=pltpu.CompilerParams(vmem_limit_bytes=8 * 2**20),
+        )(ahead, after)
 
     return jax.shard_map(
         on_device, mesh=mesh, in_specs=(placed,) * 4, out_specs=(placed, placed), check_vma=False

time: 82.2 us -> 74.3 us (0.904)
  Pallas kernels: 75.7 us -> 73.1 us
  other arithmetic: 2.37 us -> 0 us
  local copies, waits for them, and re-layouts: 2.36 us -> 0 us
    pallas_call x1 -> x2, Pallas kernels: 75.7 us -> 73.1 us  [the longest x1 71.4 us: section_of(): pl.pallas_call(functools.partial(kernel, sizes), out_shape=(whole, whole)...]
    add x1 -> x0, other arithmetic: 2.37 us -> none  [on_device(): weighted_sum + time_step / 3.0 * rates]
    unnamed x8 -> x0, local copies, waits for them, and re-layouts: 2.36 us -> none
where the time goes in v1:
time: 74.3 us; the launch traced here: 73.8 us
  Pallas kernels  73.1 us (98%)
    pallas_call x1, Pallas kernels, section_of(): pl.pallas_call(functools.partial(kernel, sizes), out_shape=(whole, whole)...  71.4 us
    pallas_call x1, Pallas kernels, on_device(): pl.pallas_call(put_out, out_shape=(ahead, after), in_specs=[pl.BlockSpec(...  1.72 us

profile of v1, /device:TPU:1, one launch (start us, length us, event | category | flops | bytes accessed | tf_op | source)
XLA Modules:
  0.0 73.8 jit_solution(11111417216306829458)
XLA Ops:
  0.6 71.4 %shard_map.59 = (f32[25,8,16,128]{3,2,1,0:T(8,128)S(1)}, f32[25,8,16,128]{3,2,1,0:T(8,128)S(1)}) custom-call(f32[25,8,16,128]{3,2,1,0:T(8,128)} %state.1, f32[25,8,16,128]{3,2,1,0:T(8,128)} %start.1, f32[25,8,16,128]{3,2,1,0:T(8,128)} %before.1, s32[3,8,16,128]{3,2,1,0:T(8,128)} %sign.1), custom_call_target="tpu_custom_call" | custom-call | tf_op jit(solution)/shard_map/pallas_call | solution.py:381
  72.0 1.7 %shard_map.60 = (f32[25,8,16,128]{3,2,1,0:T(8,128)}, f32[25,8,16,128]{3,2,1,0:T(8,128)}) custom-call(f32[25,8,16,128]{3,2,1,0:T(8,128)S(1)} %get-tuple-element.4.ahead, f32[25,8,16,128]{3,2,1,0:T(8,128)S(1)} %get-tuple-element.5.after), custom_call_target="tpu_custom_call" | custom-call | tf_op jit(solution)/shard_map/pallas_call | solution.py:433

commit v2 on v1

--- a/solution.py
+++ b/solution.py
@@ -10,8 +10,8 @@
 MESH = pl.DeviceIdType.MESH
 
 special = (0, 18, 19, 20, 21)
-early_runs = ((18, 4), (0, 1))
-middle_runs = ((14, 4), (7, 1), (1, 6))
+early_runs = ((14, 8), (0, 1))
+middle_runs = ((1, 7),)
 late_runs = ((8, 6), (22, 3))
 runs = early_runs + middle_runs + late_runs
 sym_pairs = ((0, 0), (0, 1), (0, 2), (1, 1), (1, 2), (2, 2))
@@ -22,6 +22,7 @@
 
 LAYERS = 14
 ROWS = 32
+edge_layers = (1, 2, 11, 12)
 
 
 def first_diff(at):
@@ -65,6 +66,7 @@
     y_in2,
     z_out2,
     z_in2,
+    edge,
     x_sent,
     x_got,
     n_sent,
@@ -139,7 +141,7 @@
     at_late = list(range(len(early_runs) + len(middle_runs), len(runs)))
 
     pl.semaphore_wait(barrier, 2 * len(sizes))
-    x_start(at_early)
+    x_start(at_early[:1])
 
     own.wait()
     leaning.wait()
@@ -157,6 +159,11 @@
         z_out[1, f] = turned[0:8]
 
     n_start(0)
+    for f in special:
+        for layer in edge_layers:
+            cells[f, layer, pl.ds(0, 8)] = jnp.zeros((8, 128), jnp.float32)
+            cells[f, layer, pl.ds(24, 8)] = jnp.zeros((8, 128), jnp.float32)
+    edge[...] = jnp.zeros_like(edge)
 
     @pl.loop(0, 8)
     def _(i):
@@ -166,7 +173,14 @@
             weights[3 + k, i] = dissipation / 64.0 + jnp.where(lean[k, i] == 1, scaled, -scaled)
 
     n_start(1)
-    x_start(at_middle)
+    low_half = lax.rem(here["gx"], 2) == 0
+    held = at_late[1:]
+    x_start([run for run in at_early[1:] + at_middle + at_late if run not in held])
+
+    @pl.when(jnp.logical_not(low_half))
+    def _():
+        x_start(held)
+
 
     lane = lax.broadcasted_iota(jnp.int32, (16, 128), 1)
     lane8 = lax.broadcasted_iota(jnp.int32, (8, 128), 1)
@@ -219,10 +233,17 @@
             )
 
     x_wait(at_early)
+
+    def of_xy(n, layer, rows):
+        if n == 0:
+            return 0.5 * cells[0, layer, rows] - cells[18, layer, rows]
+        return cells[18 + n, layer, rows]
+
+    for n in range(3):
+        for q, layer in enumerate(edge_layers):
+            y_out2[0, n, pl.ds(2 * q, 2)] = of_xy(n, layer, pl.ds(22, 2))
+            y_out2[1, n, pl.ds(2 * q, 2)] = of_xy(n, layer, pl.ds(8, 2))
     for n, f in enumerate(special):
-        for q, layer in enumerate((1, 2, 11, 12)):
-            y_out2[0, n, pl.ds(2 * q, 2)] = cells[f, layer, pl.ds(22, 2)]
-            y_out2[1, n, pl.ds(2 * q, 2)] = cells[f, layer, pl.ds(8, 2)]
         turned = jnp.concatenate(
             [
                 cells[f, pl.ds(1, 2), pl.ds(8, 16)].reshape(32, 128),
@@ -249,15 +270,14 @@
         drift_x(*runs[run])
 
     n_start(2)
+
+    @pl.when(low_half)
+    def _():
+        x_start(held)
+
     n_start(3)
-    x_start(at_late)
-
-    n_wait(2)
     n_wait(3)
     for n, f in enumerate(special):
-        for q, layer in enumerate((1, 2, 11, 12)):
-            cells[f, layer, pl.ds(6, 2)] = y_in2[0, n, pl.ds(2 * q, 2)]
-            cells[f, layer, pl.ds(24, 2)] = y_in2[1, n, pl.ds(2 * q, 2)]
         back = turned_back(z_in2[0, n], z_in2[1, n])
         wrap[f, pl.ds(1, 2), pl.ds(8, 16)] = back[0:32].reshape(2, 16, 128)
         wrap[f, pl.ds(11, 2), pl.ds(8, 16)] = back[32:64].reshape(2, 16, 128)
@@ -269,10 +289,6 @@
         for layer in range(3, 11):
             diff_z[n, layer, pl.ds(0, 8)] = first_diff(along_z(f, layer, 0, 8))
             diff_z[n, layer, pl.ds(24, 8)] = first_diff(along_z(f, layer, 24, 8))
-
-    for run in at_middle:
-        x_wait([run])
-        drift_x(*runs[run])
 
     @pl.loop(0, 8)
     def _(i):
@@ -318,7 +334,9 @@
         for p in range(3):
             lap_shift = hess_shift[p][0, 0] + hess_shift[p][1, 1] + hess_shift[p][2, 2]
             grad_div = hess_shift[0][0, p] + hess_shift[1][min(1, p), max(1, p)] + hess_shift[2][p, 2]
-            drive = -(4.0 / 3.0) * grad(7, p) + lap_shift + 1.0 / 3.0 * grad_div
+            drive = lap_shift + 1.0 / 3.0 * grad_div
+            if p > 0:
+                drive = drive - (4.0 / 3.0) * grad(7, p)
             add(14 + p, drive)
             add(22 + p, drive - damping * centre(22 + p))
         hess_chi = {pair: hess(0, *pair) for pair in sym_pairs}
@@ -329,7 +347,7 @@
         grad_gamma = [[grad(14 + m, k) for k in range(3)] for m in range(3)]
         ricci = []
         for s, (p, q) in enumerate(sym_pairs):
-            lap_metric = second_diff(along(1 + s, 0)) + second_diff(along(1 + s, 1)) + second_diff(along(1 + s, 2))
+            lap_metric = second_diff(along(1 + s, 1)) + second_diff(along(1 + s, 2))
             value = -0.5 * lap_metric + 0.5 * (grad_gamma[q][p] + grad_gamma[p][q]) + 0.5 * hess_chi[p, q]
             if p == q:
                 value = value + 0.5 * lap_chi
@@ -340,6 +358,21 @@
             add(8 + s, bare[s] - 1.0 / 3.0 * trace if p == q else bare[s])
         add(17, 0.5 * (ricci[0] + ricci[3] + ricci[5]) - 2.0 * kappa_one * centre(17))
 
+    x_wait(at_middle)
+    for run in at_middle:
+        drift_x(*runs[run])
+
+    @pl.loop(0, 8)
+    def _(i):
+        bent = [-0.5 * second_diff(along_x(1 + s, i)) for s in range(6)]
+        trace = bent[0] + bent[3] + bent[5]
+        for s, (p, q) in enumerate(sym_pairs):
+            rates[8 + s, i] += bent[s] - 1.0 / 3.0 * trace if p == q else bent[s]
+        rates[17, i] += 0.5 * trace
+        slope = -(4.0 / 3.0) * first_diff(along_x(7, i))
+        rates[14, i] += slope
+        rates[22, i] += slope
+
     for copy in bases:
         copy.wait()
 
@@ -365,6 +398,23 @@
             @pl.loop(0, 8, unroll=4)
             def _(i):
                 finish(f, i, rates[f, i] + drift(along_x(f, i), weights[0, i], weights[3, i]))
+
+    n_wait(2)
+
+    def corner(n):
+        for q in range(4):
+            edge[n, q, pl.ds(6, 2)] = y_in2[0, n, pl.ds(2 * q, 2)]
+            edge[n, q, pl.ds(24, 2)] = y_in2[1, n, pl.ds(2 * q, 2)]
+        outer, inner, beyond, last = [
+            first_diff(lambda m: edge[n, q, pl.ds(8 + m, 16)]) * (1.0 / 12.0) for q in range(4)
+        ]
+        return ((0, outer - 8.0 * inner), (1, inner), (6, -beyond), (7, 8.0 * beyond - last))
+
+    for n, (fields, factor) in enumerate((((9,), 1.0), ((15, 23), 1.0 / 3.0), ((14, 22), 1.0 / 3.0))):
+        for i, value in corner(n):
+            for f in fields:
+                ahead[f, i] += (time_step / 2.0 * factor) * value
+                after[f, i] += (time_step / 3.0 * factor) * value
 
     for run in range(len(runs)):
         for side in (0, 1):
@@ -397,10 +447,11 @@
             pltpu.VMEM((2, 25, 3, 8, 128), f32),
             pltpu.VMEM((2, 25, 8, 128), f32),
             pltpu.VMEM((2, 25, 8, 128), f32),
+            pltpu.VMEM((2, 3, 8, 128), f32),
+            pltpu.VMEM((2, 3, 8, 128), f32),
             pltpu.VMEM((2, 5, 8, 128), f32),
             pltpu.VMEM((2, 5, 8, 128), f32),
-            pltpu.VMEM((2, 5, 8, 128), f32),
-            pltpu.VMEM((2, 5, 8, 128), f32),
+            pltpu.VMEM((3, 4, ROWS, 128), f32),
             pltpu.SemaphoreType.DMA((2, len(runs))),
             pltpu.SemaphoreType.DMA((2, len(runs))),
             pltpu.SemaphoreType.DMA((4, 2)),

time: 74.3 us -> 72.9 us (0.981)
  Pallas kernels: 73.1 us -> 72.2 us
    pallas_call x1, Pallas kernels: 71.4 us -> 70.4 us  [section_of(): pl.pallas_call(functools.partial(kernel, sizes), out_shape=(whole, whole)...]
where the time goes in v2:
time: 72.9 us; the launch traced here: 72.8 us
  Pallas kernels  72.2 us (99%)
    pallas_call x1, Pallas kernels, section_of(): pl.pallas_call(functools.partial(kernel, sizes), out_shape=(whole, whole)...  70.4 us
    pallas_call x1, Pallas kernels, on_device(): pl.pallas_call(put_out, out_shape=(ahead, after), in_specs=[pl.BlockSpec(...  1.72 us

profile of v2, /device:TPU:1, one launch (start us, length us, event | category | flops | bytes accessed | tf_op | source)
XLA Modules:
  0.0 72.8 jit_solution(15347086745380741271)
XLA Ops:
  0.6 70.4 %shard_map.59 = (f32[25,8,16,128]{3,2,1,0:T(8,128)S(1)}, f32[25,8,16,128]{3,2,1,0:T(8,128)S(1)}) custom-call(f32[25,8,16,128]{3,2,1,0:T(8,128)} %state.1, f32[25,8,16,128]{3,2,1,0:T(8,128)} %start.1, f32[25,8,16,128]{3,2,1,0:T(8,128)} %before.1, s32[3,8,16,128]{3,2,1,0:T(8,128)} %sign.1), custom_call_target="tpu_custom_call" | custom-call | tf_op jit(solution)/shard_map/pallas_call | solution.py:431
  71.1 1.7 %shard_map.60 = (f32[25,8,16,128]{3,2,1,0:T(8,128)}, f32[25,8,16,128]{3,2,1,0:T(8,128)}) custom-call(f32[25,8,16,128]{3,2,1,0:T(8,128)S(1)} %get-tuple-element.4.ahead, f32[25,8,16,128]{3,2,1,0:T(8,128)S(1)} %get-tuple-element.5.after), custom_call_target="tpu_custom_call" | custom-call | tf_op jit(solution)/shard_map/pallas_call | solution.py:484

commit v3 on v2

--- a/solution.py
+++ b/solution.py
@@ -23,6 +23,8 @@
 LAYERS = 14
 ROWS = 32
 edge_layers = (1, 2, 11, 12)
+y_first = ((0, 8, 0), (14, 8, 8))
+y_rest = ((8, 6, 16), (22, 3, 22))
 
 
 def first_diff(at):
@@ -104,14 +106,15 @@
 
     def n_copy(which, side):
         axis, out, got = (
-            ("gy", y_out, y_in),
-            ("gz", z_out, z_in),
-            ("gy", y_out2, y_in2),
-            ("gz", z_out2, z_in2),
+            ("gy", y_out.at[side, pl.ds(0, 16)], y_in.at[side, pl.ds(0, 16)]),
+            ("gz", z_out.at[side], z_in.at[side]),
+            ("gy", y_out2.at[side], y_in2.at[side]),
+            ("gz", z_out2.at[side], z_in2.at[side]),
+            ("gy", y_out.at[side, pl.ds(16, 9)], y_in.at[side, pl.ds(16, 9)]),
         )[which]
         return pltpu.make_async_remote_copy(
-            src_ref=out.at[side],
-            dst_ref=got.at[side],
+            src_ref=out,
+            dst_ref=got,
             send_sem=n_sent.at[which, side],
             recv_sem=n_got.at[which, side],
             device_id=beside(axis, -1 if side else 1),
@@ -128,6 +131,11 @@
             for side in (0, 1):
                 x_copy(side, run).wait_recv()
 
+    def x_left(chosen):
+        for run in chosen:
+            for side in (0, 1):
+                x_copy(side, run).wait_send()
+
     def n_start(which):
         for side in (0, 1):
             n_copy(which, side).start()
@@ -146,11 +154,13 @@
     own.wait()
     leaning.wait()
 
-    @pl.loop(0, 25)
-    def _(f):
-        for r in range(3):
-            y_out[0, f, r] = cells[f, pl.ds(3, 8), 21 + r]
-            y_out[1, f, r] = cells[f, pl.ds(3, 8), 8 + r]
+    for first, count, at in y_first + y_rest:
+
+        @pl.loop(first, first + count)
+        def _(f):
+            for r in range(3):
+                y_out[0, f - first + at, r] = cells[f, pl.ds(3, 8), 21 + r]
+                y_out[1, f - first + at, r] = cells[f, pl.ds(3, 8), 8 + r]
 
     @pl.loop(0, 25)
     def _(f):
@@ -174,6 +184,11 @@
 
     n_start(1)
     low_half = lax.rem(here["gx"], 2) == 0
+
+    @pl.when(low_half)
+    def _():
+        n_start(4)
+
     held = at_late[1:]
     x_start([run for run in at_early[1:] + at_middle + at_late if run not in held])
 
@@ -212,11 +227,16 @@
         copy.start()
     n_wait(0)
 
-    @pl.loop(0, 25)
-    def _(f):
-        for r in range(3):
-            cells[f, pl.ds(3, 8), 5 + r] = y_in[0, f, r]
-            cells[f, pl.ds(3, 8), 24 + r] = y_in[1, f, r]
+    def y_place(parts):
+        for first, count, at in parts:
+
+            @pl.loop(first, first + count)
+            def _(f):
+                for r in range(3):
+                    cells[f, pl.ds(3, 8), 5 + r] = y_in[0, f - first + at, r]
+                    cells[f, pl.ds(3, 8), 24 + r] = y_in[1, f - first + at, r]
+
+    y_place(y_first)
 
     n_wait(1)
 
@@ -224,13 +244,23 @@
     def _(f):
         wrap[f, pl.ds(3, 8), pl.ds(8, 16)] = turned_back(z_in[0, f], z_in[1, f]).reshape(8, 16, 128)
 
-    @pl.loop(0, 25)
-    def _(f):
-        @pl.loop(0, 8, unroll=4)
-        def _(i):
-            rates[f, i] = drift(along_y(f, i), weights[1, i], weights[4, i]) + drift(
-                along_z(f, 3 + i, 8, 16), weights[2, i], weights[5, i]
-            )
+    for first, count, _ in y_first:
+
+        @pl.loop(first, first + count)
+        def _(f):
+            @pl.loop(0, 8, unroll=4)
+            def _(i):
+                rates[f, i] = drift(along_y(f, i), weights[1, i], weights[4, i]) + drift(
+                    along_z(f, 3 + i, 8, 16), weights[2, i], weights[5, i]
+                )
+
+    for first, count, _ in y_rest:
+
+        @pl.loop(first, first + count)
+        def _(f):
+            @pl.loop(0, 8, unroll=4)
+            def _(i):
+                rates[f, i] = drift(along_z(f, 3 + i, 8, 16), weights[2, i], weights[5, i])
 
     x_wait(at_early)
 
@@ -244,14 +274,15 @@
             y_out2[0, n, pl.ds(2 * q, 2)] = of_xy(n, layer, pl.ds(22, 2))
             y_out2[1, n, pl.ds(2 * q, 2)] = of_xy(n, layer, pl.ds(8, 2))
     for n, f in enumerate(special):
+        y_at = f - 6 if f else 0
         turned = jnp.concatenate(
             [
                 cells[f, pl.ds(1, 2), pl.ds(8, 16)].reshape(32, 128),
                 cells[f, pl.ds(11, 2), pl.ds(8, 16)].reshape(32, 128),
-                y_in[0, f, 1],
-                y_in[0, f, 2],
-                y_in[1, f, 0],
-                y_in[1, f, 1],
+                y_in[0, y_at, 1],
+                y_in[0, y_at, 2],
+                y_in[1, y_at, 0],
+                y_in[1, y_at, 1],
                 jnp.zeros((32, 128), jnp.float32),
             ],
             axis=0,
@@ -389,6 +420,21 @@
             def _(i):
                 finish(f, i, rates[f, i])
 
+    @pl.when(jnp.logical_not(low_half))
+    def _():
+        x_left(at_early + at_middle + at_late[:1])
+        n_start(4)
+
+    n_wait(4)
+    y_place(y_rest)
+    for first, count, _ in y_rest:
+
+        @pl.loop(first, first + count)
+        def _(f):
+            @pl.loop(0, 8, unroll=4)
+            def _(i):
+                rates[f, i] += drift(along_y(f, i), weights[1, i], weights[4, i])
+
     for run in at_late:
         x_wait([run])
         first, count = runs[run]
@@ -416,10 +462,12 @@
                 ahead[f, i] += (time_step / 2.0 * factor) * value
                 after[f, i] += (time_step / 3.0 * factor) * value
 
-    for run in range(len(runs)):
-        for side in (0, 1):
-            x_copy(side, run).wait_send()
-    for which in range(4):
+    @pl.when(low_half)
+    def _():
+        x_left(at_early + at_middle + at_late[:1])
+
+    x_left([run for run in range(len(runs)) if run not in at_early + at_middle + at_late[:1]])
+    for which in range(5):
         for side in (0, 1):
             n_copy(which, side).wait_send()
 
@@ -454,8 +502,8 @@
             pltpu.VMEM((3, 4, ROWS, 128), f32),
             pltpu.SemaphoreType.DMA((2, len(runs))),
             pltpu.SemaphoreType.DMA((2, len(runs))),
-            pltpu.SemaphoreType.DMA((4, 2)),
-            pltpu.SemaphoreType.DMA((4, 2)),
+            pltpu.SemaphoreType.DMA((5, 2)),
+            pltpu.SemaphoreType.DMA((5, 2)),
             pltpu.SemaphoreType.DMA((4,)),
         ],
         compiler_params=pltpu.CompilerParams(

time: 72.9 us -> 72 us (0.988)
  Pallas kernels: 72.2 us -> 71.2 us
    pallas_call x1, Pallas kernels: 70.4 us -> 69.4 us  [section_of(): pl.pallas_call(functools.partial(kernel, sizes), out_shape=(whole, whole)...]
where the time goes in v3:
time: 72 us; the launch traced here: 71.8 us
  Pallas kernels  71.2 us (99%)
    pallas_call x1, Pallas kernels, section_of(): pl.pallas_call(functools.partial(kernel, sizes), out_shape=(whole, whole)...  69.4 us
    pallas_call x1, Pallas kernels, on_device(): pl.pallas_call(put_out, out_shape=(ahead, after), in_specs=[pl.BlockSpec(...  1.72 us

profile of v3, /device:TPU:1, one launch (start us, length us, event | category | flops | bytes accessed | tf_op | source)
XLA Modules:
  0.0 71.8 jit_solution(9970229761083263187)
XLA Ops:
  0.6 69.4 %shard_map.59 = (f32[25,8,16,128]{3,2,1,0:T(8,128)S(1)}, f32[25,8,16,128]{3,2,1,0:T(8,128)S(1)}) custom-call(f32[25,8,16,128]{3,2,1,0:T(8,128)} %state.1, f32[25,8,16,128]{3,2,1,0:T(8,128)} %start.1, f32[25,8,16,128]{3,2,1,0:T(8,128)} %before.1, s32[3,8,16,128]{3,2,1,0:T(8,128)} %sign.1), custom_call_target="tpu_custom_call" | custom-call | tf_op jit(solution)/shard_map/pallas_call | solution.py:479
  70.1 1.7 %shard_map.60 = (f32[25,8,16,128]{3,2,1,0:T(8,128)}, f32[25,8,16,128]{3,2,1,0:T(8,128)}) custom-call(f32[25,8,16,128]{3,2,1,0:T(8,128)S(1)} %get-tuple-element.4.ahead, f32[25,8,16,128]{3,2,1,0:T(8,128)S(1)} %get-tuple-element.5.after), custom_call_target="tpu_custom_call" | custom-call | tf_op jit(solution)/shard_map/pallas_call | solution.py:532

commit v4 on v3

--- a/solution.py
+++ b/solution.py
@@ -431,20 +431,21 @@
 
         @pl.loop(first, first + count)
         def _(f):
-            @pl.loop(0, 8, unroll=4)
+            @pl.loop(0, 8, unroll=8)
             def _(i):
                 rates[f, i] += drift(along_y(f, i), weights[1, i], weights[4, i])
 
-    for run in at_late:
+    def close(run, together):
         x_wait([run])
         first, count = runs[run]
 
         @pl.loop(first, first + count)
         def _(f):
-            @pl.loop(0, 8, unroll=4)
+            @pl.loop(0, 8, unroll=together)
             def _(i):
                 finish(f, i, rates[f, i] + drift(along_x(f, i), weights[0, i], weights[3, i]))
 
+    close(at_late[0], 4)
     n_wait(2)
 
     def corner(n):
@@ -459,8 +460,13 @@
     for n, (fields, factor) in enumerate((((9,), 1.0), ((15, 23), 1.0 / 3.0), ((14, 22), 1.0 / 3.0))):
         for i, value in corner(n):
             for f in fields:
-                ahead[f, i] += (time_step / 2.0 * factor) * value
-                after[f, i] += (time_step / 3.0 * factor) * value
+                if f > 21:
+                    rates[f, i] += factor * value
+                else:
+                    ahead[f, i] += (time_step / 2.0 * factor) * value
+                    after[f, i] += (time_step / 3.0 * factor) * value
+
+    close(at_late[1], 8)
 
     @pl.when(low_half)
     def _():

time: 72 us -> 71.9 us (level)
  no operation moved by 1% of the time
where the time goes in v4:
time: 71.9 us; the launch traced here: 71.8 us
  Pallas kernels  71.2 us (99%)
    pallas_call x1, Pallas kernels, section_of(): pl.pallas_call(functools.partial(kernel, sizes), out_shape=(whole, whole)...  69.4 us
    pallas_call x1, Pallas kernels, on_device(): pl.pallas_call(put_out, out_shape=(ahead, after), in_specs=[pl.BlockSpec(...  1.72 us

profile of v4, /device:TPU:1, one launch (start us, length us, event | category | flops | bytes accessed | tf_op | source)
XLA Modules:
  0.0 71.8 jit_solution(962649621815799848)
XLA Ops:
  0.6 69.4 %shard_map.59 = (f32[25,8,16,128]{3,2,1,0:T(8,128)S(1)}, f32[25,8,16,128]{3,2,1,0:T(8,128)S(1)}) custom-call(f32[25,8,16,128]{3,2,1,0:T(8,128)} %state.1, f32[25,8,16,128]{3,2,1,0:T(8,128)} %start.1, f32[25,8,16,128]{3,2,1,0:T(8,128)} %before.1, s32[3,8,16,128]{3,2,1,0:T(8,128)} %sign.1), custom_call_target="tpu_custom_call" | custom-call | tf_op jit(solution)/shard_map/pallas_call | solution.py:485
  70.1 1.7 %shard_map.60 = (f32[25,8,16,128]{3,2,1,0:T(8,128)}, f32[25,8,16,128]{3,2,1,0:T(8,128)}) custom-call(f32[25,8,16,128]{3,2,1,0:T(8,128)S(1)} %get-tuple-element.4.ahead, f32[25,8,16,128]{3,2,1,0:T(8,128)S(1)} %get-tuple-element.5.after), custom_call_target="tpu_custom_call" | custom-call | tf_op jit(solution)/shard_map/pallas_call | solution.py:538
